TPU v7x, 32 devices: a whole 2x2x4 slice. The times are simulated.
32 devices in a mesh: dp: 8 (over z, y), tp: 4 (over x, core).
Axes of the slice: x: 2, y: 2, z: 4, core: 2. Of those that a mesh axis runs over, the one named last changes fastest.
Arguments:
- tokens: bfloat16 [768, 2880], P('dp', 'tp'), may hold values from -100 to 100
- attn_gain: float32 [2880], replicated, may hold values from 0.1 to 1.9
- w_query: bfloat16 [2880, 2048], P(None, 'tp'), may hold values from -0.109375 to 0.109375
- w_keyvalue: bfloat16 [2880, 8, 128], P(None, 'tp'), may hold values from -0.109375 to 0.109375
- attn_sinks: float32 [32], P('tp'), may hold values from 2 to 6
- w_out: bfloat16 [2048, 2880], P('tp'), may hold values from -0.125 to 0.125
- window_cache: bfloat16 [768, 8, 128, 128], P('dp', 'tp'), may hold values from -1000 to 1000
- positions: int32 [768], P('dp'), may hold values from 0 to 511
- moe_gain: float32 [2880], replicated, may hold values from 0.1 to 1.9
- router: bfloat16 [2880, 8], P('tp'), may hold values from -0.109375 to 0.109375
- gate_up: bfloat16 [8, 2880, 2, 2880], P('dp', None, None, 'tp'), may hold values from -0.109375 to 0.109375
- w_down: bfloat16 [8, 2880, 2880], P('dp', None, 'tp'), may hold values from -0.109375 to 0.109375
- expert_ids: int32 [768, 4], P('dp'), may hold values from 0 to 7, all different within a row; in each aligned block of 96 rows (0 to 95, 96 to 191, ...) at most 96 rows name the same one
Outputs:
- layer_out: float32 [768, 2880], P('dp', 'tp')
Inputs may be any that keep to these rules, and one draw needn't show every extreme that they name: `expert_ids`: each row names 4 different experts. Within the rows of one index of dp no expert is named by more than 96 rows, a bound that some of these blocks reach.
All inputs are finite; a program needn't handle non-finite values.
Results may differ from a plain program's by a relative error of at most 0.0066.
Values may be sent and summed in bfloat16 or wider, within the bound.
A program may use at most 128 MiB of HBM per device.

v0:
```python
import jax
import jax.numpy as jnp
from jax import lax
from jax.sharding import PartitionSpec as P

norm_eps = 1e-05
rope_base = 150000.0
glu_alpha = 1.702


def rope_tables(positions, head_size):
    half_size = head_size // 2
    exponent = jnp.arange(half_size, dtype=jnp.float32) * (2.0 / head_size)
    inverse = jnp.power(jnp.float32(rope_base), -exponent)
    angles = positions.astype(jnp.float32)[:, None] * inverse[None, :]
    return (jnp.cos(angles), jnp.sin(angles))


def rotate(values, cosine, sine_table):
    half_size = values.shape[-1] // 2
    first_half = values[..., :half_size]
    second_half = values[..., half_size:]
    return jnp.concatenate(
        [
            first_half * cosine - second_half * sine_table,
            second_half * cosine + first_half * sine_table,
        ],
        axis=-1,
    )


def on_device(
    tokens,
    attn_gain,
    w_query,
    w_keyvalue,
    attn_sinks,
    w_out,
    window_cache,
    positions,
    moe_gain,
    router,
    gate_up,
    w_down,
    expert_ids,
):
    tp_count = lax.axis_size("tp")
    dp_count = lax.axis_size("dp")
    seq_count, col_count = tokens.shape
    full_width = col_count * tp_count
    col_start = lax.axis_index("tp") * col_count
    head_size = w_keyvalue.shape[2] // 2
    kv_local = w_keyvalue.shape[1]
    q_local = w_query.shape[1] // head_size
    group_size = q_local // kv_local
    window = window_cache.shape[2]
    attn_slice = lax.dynamic_slice_in_dim(attn_gain, col_start, col_count)
    moe_slice = lax.dynamic_slice_in_dim(moe_gain, col_start, col_count)
    tok_wide = tokens.astype(jnp.float32)
    attn_sq = lax.psum(jnp.sum(tok_wide * tok_wide, axis=1), "tp")
    normed = (
        tok_wide * lax.rsqrt(attn_sq / full_width + norm_eps)[:, None] * attn_slice[None, :]
    ).astype(jnp.bfloat16)
    kv_flat = w_keyvalue.reshape(full_width, kv_local * 2 * head_size)
    piece_rows = lax.all_gather(normed, "tp", axis=1, tiled=True)
    queries = jnp.dot(piece_rows, w_query, preferred_element_type=jnp.float32)
    fresh_rows = jnp.dot(piece_rows, kv_flat, preferred_element_type=jnp.float32)
    cosine, sine_table = rope_tables(positions, head_size)
    rot_queries = rotate(
        queries.reshape(seq_count, q_local, head_size), cosine[:, None, :], sine_table[:, None, :]
    ).astype(jnp.bfloat16)
    fresh_rows = fresh_rows.reshape(seq_count, kv_local, 2 * head_size)
    new_key = rotate(fresh_rows[..., :head_size], cosine[:, None, :], sine_table[:, None, :])
    new_entry = jnp.concatenate([new_key, fresh_rows[..., head_size:]], axis=-1).astype(
        jnp.bfloat16
    )
    slot_ids = jnp.arange(window, dtype=jnp.int32)
    is_current = slot_ids[None, :] == (positions % window)[:, None]
    cache_now = jnp.where(is_current[:, None, :, None], new_entry[:, :, None, :], window_cache)
    is_valid = (positions[:, None] - slot_ids[None, :]) % window <= positions[:, None]
    grouped = rot_queries.reshape(seq_count, kv_local, group_size, head_size)
    scores = jnp.einsum(
        "skgh,skwh->skgw", grouped, cache_now[..., :head_size], preferred_element_type=jnp.float32
    ) * head_size ** (-0.5)
    scores = jnp.where(is_valid[:, None, None, :], scores, -jnp.inf)
    sink_col = attn_sinks.reshape(kv_local, group_size)[None, :, :, None]
    peak_score = jnp.maximum(jnp.max(scores, axis=-1, keepdims=True), sink_col)
    raised = jnp.exp(scores - peak_score)
    denominator = jnp.sum(raised, axis=-1, keepdims=True) + jnp.exp(sink_col - peak_score)
    prob_bf = (raised / denominator).astype(jnp.bfloat16)
    attended = jnp.einsum(
        "skgw,skwh->skgh", prob_bf, cache_now[..., head_size:], preferred_element_type=jnp.float32
    ).astype(jnp.bfloat16)
    partial_out = jnp.dot(
        attended.reshape(seq_count, q_local * head_size), w_out, preferred_element_type=jnp.float32
    )
    residual = tok_wide + lax.psum_scatter(
        partial_out.astype(jnp.bfloat16), "tp", scatter_dimension=1, tiled=True
    ).astype(jnp.float32)
    experts = router.shape[1]
    top_count = expert_ids.shape[1]
    local_experts = gate_up.shape[0]
    ff_local = gate_up.shape[3]
    capacity = min(seq_count, max(2, 8 * seq_count * top_count // (3 * experts)))
    moe_sq = jnp.sum(residual * residual, axis=1)
    router_wide = router.astype(jnp.float32)
    total_sq = lax.psum(moe_sq, "tp")
    moe_scale = lax.rsqrt(total_sq / full_width + norm_eps)[:, None]
    scaled = residual * moe_scale * moe_slice[None, :]
    logits = lax.psum(jnp.dot(scaled, router_wide, precision=lax.Precision.HIGHEST), "tp")
    hidden_rows = scaled.astype(jnp.bfloat16)
    expert_iota = jnp.arange(experts, dtype=jnp.int32)
    chosen = expert_ids[:, :, None] == expert_iota[None, None, :]
    picked = jnp.sum(jnp.where(chosen, logits[:, None, :], 0.0), axis=-1)
    raised_logits = jnp.exp(picked)
    route_weights = raised_logits / jnp.sum(raised_logits, axis=1, keepdims=True)
    assign = expert_ids.reshape(-1)
    onehot = (assign[:, None] == expert_iota[None, :]).astype(jnp.int32)
    earlier = jnp.cumsum(onehot, axis=0) - onehot
    slot_of = jnp.sum(earlier * onehot, axis=1)
    target = (assign * capacity + slot_of).reshape(seq_count, top_count)
    spot_ids = jnp.arange(experts * capacity, dtype=jnp.int32)
    slot_hits = target[:, :, None] == spot_ids[None, None, :]
    placer = jnp.transpose(jnp.any(slot_hits, axis=1)).astype(jnp.bfloat16)
    combiner = jnp.sum(jnp.where(slot_hits, route_weights[:, :, None], 0.0), axis=1)
    gate_up_flat = gate_up.reshape(local_experts, full_width, 2 * ff_local)
    placed = jnp.dot(placer, hidden_rows, preferred_element_type=jnp.float32).astype(jnp.bfloat16)
    mixed_in = jnp.einsum(
        "gecd,edf->gecf",
        lax.all_gather(
            lax.all_to_all(
                placed.reshape(dp_count, local_experts, capacity, hidden_rows.shape[1]),
                "dp",
                split_axis=0,
                concat_axis=0,
                tiled=True,
            ),
            "tp",
            axis=3,
            tiled=True,
        ),
        gate_up_flat,
        preferred_element_type=jnp.float32,
    )
    gate_part = mixed_in[..., :ff_local]
    up_part = mixed_in[..., ff_local:]
    act_rows = (gate_part * jax.nn.sigmoid(glu_alpha * gate_part) * (up_part + 1.0)).astype(
        jnp.bfloat16
    )
    answered = jnp.einsum(
        "gecf,efd->gecd",
        lax.all_gather(act_rows, "tp", axis=3, tiled=True),
        w_down,
        preferred_element_type=jnp.float32,
    ).astype(jnp.bfloat16)
    returned = lax.all_to_all(answered, "dp", split_axis=0, concat_axis=0, tiled=True)
    flat_back = returned.reshape(experts * capacity, col_count).astype(jnp.float32)
    moe_out = jnp.dot(combiner, flat_back, precision=lax.Precision.HIGHEST)
    return residual + moe_out


def solution(mesh):
    in_specs = (
        P("dp", "tp"),
        P(),
        P(None, "tp"),
        P(None, "tp", None),
        P("tp"),
        P("tp", None),
        P("dp", "tp", None, None),
        P("dp"),
        P(),
        P("tp", None),
        P("dp", None, None, "tp"),
        P("dp", None, "tp"),
        P("dp", None),
    )
    out_specs = P("dp", "tp")
    return jax.shard_map(
        on_device, mesh=mesh, in_specs=in_specs, out_specs=out_specs, check_vma=False
    )
```

profile of v0, /device:TPU:0, one launch (start us, length us, event | category | flops | bytes accessed | tf_op | source)
XLA Modules:
  0.0 306.0 jit_solution(1373459359515891442)
XLA Ops:
  6.6 1.2 fusion.37
  7.8 8.4 %psum.21 = f32[96]{0:T(128)S(1)} all-reduce(f32[96]{0:T(128)S(1)} %fusion.37), channel_id=1, replica_groups=mesh['dp'=8,'tp'=4] {'tp'}, use_global_device_ids=true, to_apply=%region_1.0 | all-reduce | flops 96 | bytes 768 | tf_op jit(solution)/shard_map/psum | solution.py:60
  16.1 0.8 dynamic_slice.6
  16.9 1.0 fusion.48
  17.9 6.7 %all-gather = bf16[4,720,96]{1,2,0:T(8,128)(2,1)S(1)} all-gather(bf16[1,720,96]{1,2,0:T(8,128)(2,1)S(1)} %fusion.48), channel_id=1, replica_groups=mesh['dp'=8,'tp'=4] {'tp'}, dimensions={0}, use_global_device_ids=true | all-gather | bytes 691200 | tf_op jit(solution)/shard_map/all_gather | solution.py:65
  24.6 0.5 copy.86
  25.1 1.3 reshape.248
  26.4 1.3 reshape.247
  27.6 0.5 fusion.63
  28.2 0.7 fusion.54
  28.9 4.9 %copy.111 = bf16[2880,2,128]{0,2,1:T(8,128)(2,1)} copy(bf16[2880,2,128]{2,1,0:T(2,128)(2,1)} %param.16) | data formatting | bytes 2949120 | tf_op jit(solution)/shard_map/dot_general | solution.py:67
  33.7 0.1 multiply_cosine_fusion
  33.9 0.7 copy.92
  34.6 0.7 copy.93
  35.3 2.0 fusion.19
  37.3 0.1 slice.84
  37.4 0.9 subtract_convert_fusion.1
  38.3 0.1 pad_maximum_fusion
  38.4 0.7 copy.94
  39.1 1.3 iota_compare_fusion.1
  40.4 8.7 %copy.95 = bf16[96,2,128,128]{2,3,1,0:T(8,128)(2,1)} copy(bf16[96,2,128,128]{3,2,1,0:T(8,128)(2,1)} %param.19) | data formatting | bytes 12582912 | tf_op args[6]
  49.1 3.1 %fusion.65 = f32[96,512]{0,1:T(8,128)S(1)} fusion(bf16[2880,96]{0,1:T(8,128)(2,1)S(1)} %copy-done.3, bf16[2880,512]{1,0:T(8,128)(2,1)} %param.15), kind=kOutput, calls=%fused_computation.91 | convolution fusion | flops 283115520 | bytes 3698688 | tf_op jit(solution)/shard_map/dot_general | solution.py:66
  52.3 0.2 copy.88
  52.4 0.2 copy.89
  52.6 0.1 max.18
  52.7 7.2 %broadcast_select_fusion = bf16[96,2,128,128]{2,3,1,0:T(8,128)(2,1)S(1)} fusion(bf16[96,2,128,128]{2,3,1,0:T(8,128)(2,1)} %copy.95, pred[96,128]{1,0:T(8,128)(4,1)} %iota_compare_fusion.1, bf16[96,2,128]{2,1,0:T(2,128)(2,1)} %copy.94), kind=kLoop, calls=%fused_computation | loop fusion | flops 3145728 | bytes 12644352 | tf_op jit(solution)/shard_map/jit(_where)/select_n | solution.py:79
  59.9 1.2 fusion.64
  61.2 0.6 fusion.36
  61.8 1.8 fusion.33
  63.6 0.2 copy.96
  63.8 1.9 convolution_convert_fusion
  65.7 2.2 copy.112
  68.0 0.1 copy.97
  68.1 0.1 eq.76
  68.2 0.1 eq.72
  68.3 0.8 dynamic_slice.7
  69.1 0.8 reduce-window.6
  69.9 0.2 slice_reduce_fusion
  70.2 0.1 fusion.59
  70.3 0.1 reduce_sum.68
  70.5 0.2 fusion.32
  70.7 21.4 %reduce-scatter.4.cloned.1.call-done = bf16[720,96]{1,0:T(8,128)(2,1)} async-done(((bf16[2880,96]{1,0:T(8,128)(2,1)}), bf16[720,96]{1,0:T(8,128)(2,1)}) %reduce-scatter.4.cloned.1.call-update) | async-done | bytes 138256
  92.1 1.0 copy.113
  93.2 0.1 multiply_reduce_fusion
  93.3 5.8 %psum.22 = f32[96]{0:T(128)S(1)} all-reduce(f32[96]{0:T(128)S(1)} %multiply_reduce_fusion), channel_id=1, replica_groups=mesh['dp'=8,'tp'=4] {'tp'}, use_global_device_ids=true, to_apply=%region_9.10 | all-reduce | flops 96 | bytes 768 | tf_op jit(solution)/shard_map/psum | solution.py:107
  99.1 0.6 convolution_convert_fusion.1
  99.7 0.6 copy.100
  100.3 34.2 %all_to_all.10 = bf16[8,1,96,720]{3,2,1,0:T(8,128)(2,1)S(1)} all-to-all(bf16[8,1,96,720]{3,2,1,0:T(8,128)(2,1)S(1)} %bitcast.88), channel_id=1, replica_groups=mesh['dp'=8,'tp'=4] {'dp'}, dimensions={0} | all-to-all | bytes 2211840 | tf_op jit(solution)/shard_map/all_to_all | solution.py:131
  134.5 1.9 copy.102
  136.5 0.2 all-gather.6.cloned.1.call-start
  136.7 41.8 %all-gather.4.cloned.1.call-done = bf16[8,1,96,2880]{2,0,1,3:T(8,128)(2,1)} async-done(((bf16[8,1,96,720]{2,0,1,3:T(8,128)(2,1)}), bf16[8,1,96,2880]{2,0,1,3:T(8,128)(2,1)}) %all-gather.4.cloned.1.call-update) | async-done | bytes 4423696 | tf_op jit(solution)/shard_map/all_gather | solution.py:130
  178.5 8.3 %copy.103 = bf16[8,1,96,2880]{3,2,0,1:T(8,128)(2,1)} copy(bf16[8,1,96,2880]{2,0,1,3:T(8,128)(2,1)} %all-gather.4.cloned.1.call-done) | data formatting | bytes 8847360 | tf_op jit(solution)/shard_map/all_gather | solution.py:130
  186.8 11.4 %fusion.5 = f32[8,1,96,1440]{3,2,0,1:T(8,128)S(1)} fusion(bf16[2880,1440,1]{0,1,2:T(8,128)(2,1)} %bitcast.104, bf16[8,1,96,2880]{3,2,0,1:T(8,128)(2,1)} %copy.103), kind=kOutput, calls=%fused_computation.6 | convolution fusion | flops 6370099200 | bytes 17141760 | tf_op jit(solution)/shard_map/gecd,edf->gecf/dot_general | solution.py:128
  198.2 0.8 fusion.13
  199.1 1.9 copy.104
  201.0 44.3 %all-gather.6.cloned.1.call-done = bf16[8,1,96,2880]{2,0,1,3:T(8,128)(2,1)} async-done(((bf16[8,1,96,720]{2,0,1,3:T(8,128)(2,1)}), bf16[8,1,96,2880]{2,0,1,3:T(8,128)(2,1)}) %all-gather.6.cloned.1.call-update) | async-done | bytes 4423696 | tf_op jit(solution)/shard_map/all_gather | solution.py:152
  245.3 8.3 %copy.105 = bf16[8,1,96,2880]{3,2,0,1:T(8,128)(2,1)} copy(bf16[8,1,96,2880]{2,0,1,3:T(8,128)(2,1)} %all-gather.6.cloned.1.call-done) | data formatting | bytes 8847360 | tf_op jit(solution)/shard_map/all_gather | solution.py:152
  253.6 8.6 %fusion.21 = bf16[8,1,96,720]{3,2,1,0:T(8,128)(2,1)} fusion(bf16[1,2880,720]{1,2,0:T(8,128)(2,1)} %param.24, bf16[8,1,96,2880]{3,2,0,1:T(8,128)(2,1)} %copy.105), kind=kOutput, calls=%fused_computation.19 | convolution fusion | flops 3185602560 | bytes 9676800 | tf_op jit(solution)/shard_map/gecf,efd->gecd/dot_general | solution.py:150
  262.2 5.5 %all-to-all-start.1 = ((bf16[8,1,96,720]{3,2,1,0:T(8,128)(2,1)}), bf16[8,1,96,720]{3,2,1,0:T(8,128)(2,1)}, u32[]{:S(2)}, u32[]{:S(2)}) async-start(bf16[8,1,96,720]{3,2,1,0:T(8,128)(2,1)} %fusion.21), calls=%async_computation.1 | async-start | bytes 2359296 | tf_op jit(solution)/shard_map/all_to_all | solution.py:156
  267.7 0.3 fusion.41
  268.0 6.2 %psum.23 = f32[96,8]{0,1:T(8,128)S(1)} all-reduce(f32[96,8]{0,1:T(8,128)S(1)} %fusion.41), channel_id=1, replica_groups=mesh['dp'=8,'tp'=4] {'tp'}, use_global_device_ids=true, to_apply=%region_10.11 | all-reduce | flops 768 | bytes 6144 | tf_op jit(solution)/shard_map/psum | solution.py:110
  274.3 0.2 select_reduce_fusion
  274.5 22.3 %all-to-all-done.1 = bf16[8,1,96,720]{3,2,1,0:T(8,128)(2,1)} async-done(((bf16[8,1,96,720]{3,2,1,0:T(8,128)(2,1)}), bf16[8,1,96,720]{3,2,1,0:T(8,128)(2,1)}, u32[]{:S(2)}, u32[]{:S(2)}) %all-to-all-start.1) | async-done | bytes 1105952 | tf_op jit(solution)/shard_map/all_to_all | solution.py:156
  296.8 2.7 convolution_add_fusion
  (40 shorter events, 0.4 us)
Async XLA Ops:
  6.5 57.3 %copy-start = (bf16[512,2880]{0,1:T(8,128)(2,1)S(1)}, bf16[512,2880]{0,1:T(8,128)(2,1)}, u32[]{:S(2)}) copy-start(bf16[512,2880]{0,1:T(8,128)(2,1)} %param.18) | copy-start | bytes 8847364
  6.5 21.1 %copy-start.7 = (s32[96]{0:T(128)S(1)}, s32[96]{0:T(128)}, u32[]{:S(2)}) copy-start(s32[96]{0:T(128)} %param.20) | copy-start | bytes 1156
  6.5 85.6 %reduce-scatter.4.cloned.1.call-start = ((), (), s32[]{:S(2)}) async-start(), calls=%async_computation.5 | async-start | bytes 921600
  27.6 7.7 %copy-start.4 = (bf16[2880,96,1]{0,1,2:T(8,128)(2,1)S(1)}, bf16[2880,96,1]{0,1,2:T(8,128)(2,1)}, u32[]{:S(2)}) copy-start(bf16[2880,96,1]{0,1,2:T(8,128)(2,1)} %reshape.248) | copy-start | bytes 1658884
  40.4 8.7 %copy-start.3 = (bf16[2880,96]{0,1:T(8,128)(2,1)S(1)}, bf16[2880,96]{0,1:T(8,128)(2,1)}, u32[]{:S(2)}) copy-start(bf16[2880,96]{0,1:T(8,128)(2,1)} %reshape.247) | copy-start | bytes 1658884
  49.1 3.5 %copy-start.9 = (f32[8]{0:T(128)S(1)}, f32[8]{0:T(128)}, u32[]{:S(2)}) copy-start(f32[8]{0:T(128)} %param.17) | copy-start | bytes 100
  52.7 7.2 %copy-start.6 = (pred[96,128]{1,0:T(8,128)(4,1)S(1)}, pred[96,128]{1,0:T(8,128)(4,1)}, u32[]{:S(2)}) copy-start(pred[96,128]{1,0:T(8,128)(4,1)} %fusion.54) | copy-start | bytes 36868
  63.6 4.4 %copy-start.5 = (s32[96,4]{0,1:T(4,128)S(1)}, s32[96,4]{0,1:T(4,128)}, u32[]{:S(2)}) copy-start(s32[96,4]{0,1:T(4,128)} %param.25) | copy-start | bytes 4612
  63.8 29.4 %copy-start.2 = (bf16[96,720]{1,0:T(8,128)(2,1)S(1)}, bf16[96,720]{1,0:T(8,128)(2,1)}, u32[]{:S(2)}) copy-start(bf16[96,720]{1,0:T(8,128)(2,1)} %param.13) | copy-start | bytes 414724
  67.9 110.5 %all-gather.4.cloned.1.call-start = ((), (), s32[]{:S(2)}) async-start(), calls=%async_computation.3 | async-start | bytes 7372800 | tf_op jit(solution)/shard_map/all_gather | solution.py:130
  136.5 108.8 %all-gather.6.cloned.1.call-start = ((), (), s32[]{:S(2)}) async-start(), calls=%async_computation.4 | async-start | bytes 7372800 | tf_op jit(solution)/shard_map/all_gather | solution.py:152
  253.6 14.1 %copy-start.8 = (bf16[720,8]{0,1:T(8,128)(2,1)S(1)}, bf16[720,8]{0,1:T(8,128)(2,1)}, u32[]{:S(2)}) copy-start(bf16[720,8]{0,1:T(8,128)(2,1)} %param.22) | copy-start | bytes 34564
  253.6 45.9 %copy-start.1 = (bf16[512,2880]{0,1:T(8,128)(2,1)S(1)}, bf16[512,2880]{0,1:T(8,128)(2,1)}, u32[]{:S(2)}) copy-start(bf16[512,2880]{0,1:T(8,128)(2,1)} %param.18) | copy-start | bytes 8847364
  262.2 34.6 %all-to-all-start.1 = ((bf16[8,1,96,720]{3,2,1,0:T(8,128)(2,1)}), bf16[8,1,96,720]{3,2,1,0:T(8,128)(2,1)}, u32[]{:S(2)}, u32[]{:S(2)}) async-start(bf16[8,1,96,720]{3,2,1,0:T(8,128)(2,1)} %fusion.21), calls=%async_computation.1 | async-start | bytes 2359296 | tf_op jit(solution)/shard_map/all_to_all | solution.py:156
Sparse Core Ops, SparseCore 0:
  68.0 24.0 reduce-scatter.3
  136.6 41.8 all-gather.3
  201.1 44.1 all-gather.5
where the time goes:
time: 307 us; the launch traced here: 306 us
  waiting for transfers between devices  130 us (42%)
  blocking collectives  61.2 us (20%)
  local copies, waits for them, and re-layouts  46.1 us (15%)
  matrix products  33.5 us (11%)
  other arithmetic  16.2 us (5%)
  between operations  13.4 us (4%)
  starting transfers between devices  5.78 us (2%)
    all_gather x1, waiting for transfers between devices, on_device(): lax.all_gather(act_rows, 'tp', axis=3, tiled=True)  44.3 us
    all_gather x1, waiting for transfers between devices, on_device(): lax.all_gather(lax.all_to_all(placed.reshape(dp_count, local_experts, cap...  41.8 us
    all_to_all x1, blocking collectives, on_device(): lax.all_to_all(placed.reshape(dp_count, local_experts, capacity, hidden_r...  34.2 us
    all_to_all x1, waiting for transfers between devices, on_device(): lax.all_to_all(answered, 'dp', split_axis=0, concat_axis=0, tiled=True)  22.3 us
    unnamed x4, waiting for transfers between devices  21.5 us
    unnamed x28, local copies, waits for them, and re-layouts  14.7 us
    dot_general x1, matrix products, on_device(): jnp.einsum('gecd,edf->gecf', lax.all_gather(lax.all_to_all(placed.reshape...  11.4 us
    dot_general x1, matrix products, on_device(): jnp.einsum('gecf,efd->gecd', lax.all_gather(act_rows, 'tp', axis=3, tiled...  8.57 us
  transfers between devices with their start and end apart: 4, of which 4 were waited for; matrix products, arithmetic and copies ran while one was open for 1% of the time, Pallas kernels for 0%

commit v1 on v0

--- a/solution.py
+++ b/solution.py
@@ -2,10 +2,27 @@
 import jax.numpy as jnp
 from jax import lax
 from jax.sharding import PartitionSpec as P
+from jax.lax import axis_index, axis_size, ppermute
 
 norm_eps = 1e-05
 rope_base = 150000.0
 glu_alpha = 1.702
+
+
+def teams_run(z_in, block_in):
+    ready, block_out, moved = (axis_size("tp"), axis_index("tp"), z_in.shape[3])
+    rows = [(it, (it + 1) % ready) for it in range(ready)]
+    sheets = [(it, (it - 1) % ready) for it in range(ready)]
+    h_now = ready // 2
+    answer = block_in(z_in, block_out * moved)
+    n_now = high = z_in
+    for p in tuple(range(1, h_now + 1)):
+        n_now = ppermute(n_now, axis_name="tp", perm=rows)
+        if p < ready - h_now:
+            high = ppermute(high, axis_name="tp", perm=sheets)
+            answer = answer + block_in(high, (block_out + p) % ready * moved)
+        answer = answer + block_in(n_now, (block_out - p) % ready * moved)
+    return answer
 
 
 def rope_tables(positions, head_size):
@@ -147,11 +164,14 @@
     act_rows = (gate_part * jax.nn.sigmoid(glu_alpha * gate_part) * (up_part + 1.0)).astype(
         jnp.bfloat16
     )
-    answered = jnp.einsum(
-        "gecf,efd->gecd",
-        lax.all_gather(act_rows, "tp", axis=3, tiled=True),
-        w_down,
-        preferred_element_type=jnp.float32,
+    answered = teams_run(
+        act_rows,
+        lambda shard, offset: jnp.einsum(
+            "gecf,efd->gecd",
+            shard,
+            lax.dynamic_slice_in_dim(w_down, offset, shard.shape[3], axis=1),
+            preferred_element_type=jnp.float32,
+        ),
     ).astype(jnp.bfloat16)
     returned = lax.all_to_all(answered, "dp", split_axis=0, concat_axis=0, tiled=True)
     flat_back = returned.reshape(experts * capacity, col_count).astype(jnp.float32)

time: 307 us -> 289 us (0.941)
  waiting for transfers between devices: 130 us -> 117 us
  local copies, waits for them, and re-layouts: 46.1 us -> 35.8 us
  matrix products: 33.5 us -> 37 us
    all_gather x1 -> x0, waiting for transfers between devices: 44.3 us -> none  [on_device(): lax.all_gather(act_rows, 'tp', axis=3, tiled=True)]
    ppermute x0 -> x3, waiting for transfers between devices: none -> 33.7 us  [the longest x2 33.7 us: teams_run(): n_now = ppermute(n_now, axis_name='tp', perm=rows)]
    all_gather x1 -> x0, local copies, waits for them, and re-layouts: 8.35 us -> none  [on_device(): lax.all_gather(act_rows, 'tp', axis=3, tiled=True)]
    dot_general x1 -> x4, matrix products: 8.57 us -> 12 us  [on_device(): jnp.einsum('gecf,efd->gecd', shard, lax.dynamic_slice_in_dim(w_down, offs...]
    unnamed x4 -> x3, waiting for transfers between devices: 21.5 us -> 21.4 us
  transfers between devices with their start and end apart: 4 -> 6, of which waited for: 4 -> 5; matrix products, arithmetic and copies ran while one was open for 1% -> 4% of each run, Pallas kernels for 0% -> 0%
where the time goes in v1:
time: 289 us; the launch traced here: 288 us
  waiting for transfers between devices  117 us (40%)
  blocking collectives  61.1 us (21%)
  matrix products  37 us (13%)
  local copies, waits for them, and re-layouts  35.8 us (12%)
  other arithmetic  16.2 us (6%)
  between operations  13.7 us (5%)
  starting transfers between devices  7.28 us (3%)
    all_gather x1, waiting for transfers between devices, on_device(): lax.all_gather(lax.all_to_all(placed.reshape(dp_count, local_experts, cap...  42 us
    all_to_all x1, blocking collectives, on_device(): lax.all_to_all(placed.reshape(dp_count, local_experts, capacity, hidden_r...  34.2 us
    ppermute x2, waiting for transfers between devices, teams_run(): n_now = ppermute(n_now, axis_name='tp', perm=rows)  33.7 us
    unnamed x3, waiting for transfers between devices  21.4 us
    all_to_all x1, waiting for transfers between devices, on_device(): lax.all_to_all(answered, 'dp', split_axis=0, concat_axis=0, tiled=True)  19.6 us
    unnamed x28, local copies, waits for them, and re-layouts  14.7 us
    dot_general x4, matrix products, on_device(): jnp.einsum('gecf,efd->gecd', shard, lax.dynamic_slice_in_dim(w_down, offs...  12 us
    dot_general x1, matrix products, on_device(): jnp.einsum('gecd,edf->gecf', lax.all_gather(lax.all_to_all(placed.reshape...  11.4 us
  transfers between devices with their start and end apart: 6, of which 5 were waited for; matrix products, arithmetic and copies ran while one was open for 4% of the time, Pallas kernels for 0%

profile of v1, /device:TPU:0, one launch (start us, length us, event | category | flops | bytes accessed | tf_op | source)
XLA Modules:
  0.0 287.8 jit_solution(7466907026957487872)
XLA Ops:
  6.6 1.2 fusion.40
  7.8 8.4 %psum.21 = f32[96]{0:T(128)S(1)} all-reduce(f32[96]{0:T(128)S(1)} %fusion.40), channel_id=1, replica_groups=mesh['dp'=8,'tp'=4] {'tp'}, use_global_device_ids=true, to_apply=%region_1.0 | all-reduce | flops 96 | bytes 768 | tf_op jit(solution)/shard_map/psum | solution.py:77
  16.1 0.8 dynamic_slice.18
  16.9 1.0 fusion.51
  17.9 6.7 %all-gather = bf16[4,720,96]{1,2,0:T(8,128)(2,1)S(1)} all-gather(bf16[1,720,96]{1,2,0:T(8,128)(2,1)S(1)} %fusion.51), channel_id=1, replica_groups=mesh['dp'=8,'tp'=4] {'tp'}, dimensions={0}, use_global_device_ids=true | all-gather | bytes 691200 | tf_op jit(solution)/shard_map/all_gather | solution.py:82
  24.6 0.5 copy.98
  25.1 1.3 reshape.278
  26.4 1.3 reshape.277
  27.6 0.5 fusion.70
  28.2 0.7 fusion.57
  28.9 4.9 %copy.125 = bf16[2880,2,128]{0,2,1:T(8,128)(2,1)} copy(bf16[2880,2,128]{2,1,0:T(2,128)(2,1)} %param.16) | data formatting | bytes 2949120 | tf_op jit(solution)/shard_map/dot_general | solution.py:84
  33.8 0.1 multiply_cosine_fusion
  33.9 0.7 copy.104
  34.6 0.7 copy.105
  35.3 2.0 fusion.11
  37.4 0.9 subtract_convert_fusion.1
  38.3 0.1 pad_maximum_fusion
  38.4 0.7 copy.106
  39.1 1.3 iota_compare_fusion.1
  40.4 8.7 %copy.107 = bf16[96,2,128,128]{2,3,1,0:T(8,128)(2,1)} copy(bf16[96,2,128,128]{3,2,1,0:T(8,128)(2,1)} %param.19) | data formatting | bytes 12582912 | tf_op args[6]
  49.1 3.1 %fusion.72 = f32[96,512]{0,1:T(8,128)S(1)} fusion(bf16[2880,96]{0,1:T(8,128)(2,1)S(1)} %copy-done.3, bf16[2880,512]{1,0:T(8,128)(2,1)} %param.15), kind=kOutput, calls=%fused_computation.107 | convolution fusion | flops 283115520 | bytes 3698688 | tf_op jit(solution)/shard_map/dot_general | solution.py:83
  52.3 0.2 copy.100
  52.4 0.2 copy.101
  52.7 7.2 %broadcast_select_fusion = bf16[96,2,128,128]{2,3,1,0:T(8,128)(2,1)S(1)} fusion(bf16[96,2,128,128]{2,3,1,0:T(8,128)(2,1)} %copy.107, pred[96,128]{1,0:T(8,128)(4,1)} %iota_compare_fusion.1, bf16[96,2,128]{2,1,0:T(2,128)(2,1)} %copy.106), kind=kLoop, calls=%fused_computation | loop fusion | flops 3145728 | bytes 12644352 | tf_op jit(solution)/shard_map/jit(_where)/select_n | solution.py:96
  59.9 1.2 fusion.71
  61.2 0.6 fusion.39
  61.8 1.8 fusion.28
  63.6 0.2 copy.108
  63.8 1.9 convolution_convert_fusion
  65.7 2.2 copy.126
  68.0 0.1 copy.109
  68.1 0.1 eq.80
  68.2 0.1 eq.76
  68.3 0.8 dynamic_slice.19
  69.1 0.8 reduce-window.6
  69.9 0.2 slice_reduce_fusion
  70.3 0.1 reduce_sum.68
  70.5 0.2 fusion.27
  70.7 21.4 %reduce-scatter.4.cloned.1.call-done = bf16[720,96]{1,0:T(8,128)(2,1)} async-done(((bf16[2880,96]{1,0:T(8,128)(2,1)}), bf16[720,96]{1,0:T(8,128)(2,1)}) %reduce-scatter.4.cloned.1.call-update) | async-done | bytes 138256
  92.2 1.0 copy.127
  93.2 0.1 multiply_reduce_fusion
  93.4 5.8 %psum.22 = f32[96]{0:T(128)S(1)} all-reduce(f32[96]{0:T(128)S(1)} %multiply_reduce_fusion), channel_id=1, replica_groups=mesh['dp'=8,'tp'=4] {'tp'}, use_global_device_ids=true, to_apply=%region_9.10 | all-reduce | flops 96 | bytes 768 | tf_op jit(solution)/shard_map/psum | solution.py:124
  99.1 0.6 convolution_convert_fusion.1
  99.7 0.6 copy.113
  100.4 34.2 %all_to_all.10 = bf16[8,1,96,720]{3,2,1,0:T(8,128)(2,1)S(1)} all-to-all(bf16[8,1,96,720]{3,2,1,0:T(8,128)(2,1)S(1)} %bitcast.103), channel_id=1, replica_groups=mesh['dp'=8,'tp'=4] {'dp'}, dimensions={0} | all-to-all | bytes 2211840 | tf_op jit(solution)/shard_map/all_to_all | solution.py:148
  134.6 1.9 copy.115
  136.5 42.0 %all-gather.3.cloned.1.call-done = bf16[8,1,96,2880]{2,0,1,3:T(8,128)(2,1)} async-done(((bf16[8,1,96,720]{2,0,1,3:T(8,128)(2,1)}), bf16[8,1,96,2880]{2,0,1,3:T(8,128)(2,1)}) %all-gather.3.cloned.1.call-update) | async-done | bytes 4423696 | tf_op jit(solution)/shard_map/all_gather | solution.py:147
  178.5 8.3 %copy.116 = bf16[8,1,96,2880]{3,2,0,1:T(8,128)(2,1)} copy(bf16[8,1,96,2880]{2,0,1,3:T(8,128)(2,1)} %all-gather.3.cloned.1.call-done) | data formatting | bytes 8847360 | tf_op jit(solution)/shard_map/all_gather | solution.py:147
  186.8 11.4 %fusion.2 = f32[8,1,96,1440]{3,2,0,1:T(8,128)S(1)} fusion(bf16[2880,1440,1]{0,1,2:T(8,128)(2,1)} %bitcast.119, bf16[8,1,96,2880]{3,2,0,1:T(8,128)(2,1)} %copy.116), kind=kOutput, calls=%fused_computation.3 | convolution fusion | flops 6370099200 | bytes 17141760 | tf_op jit(solution)/shard_map/gecd,edf->gecf/dot_general | solution.py:145
  198.2 0.8 fusion.10
  199.1 0.3 collective-permute-start.1
  199.4 1.5 collective-permute-start
  200.9 25.9 %collective-permute-done.1 = bf16[8,1,96,720]{3,2,0,1:T(8,128)(2,1)S(1)} collective-permute-done((bf16[8,1,96,720]{3,2,0,1:T(8,128)(2,1)S(1)}, bf16[8,1,96,720]{3,2,0,1:T(8,128)(2,1)S(1)}, u32[]{:S(2)}, u32[]{:S(2)}) %collective-permute-start.1) | collective-permute-done | bytes 1105952 | tf_op jit(solution)/shard_map/ppermute | solution.py:20
  226.8 2.5 fusion.25
  229.3 2.5 fusion.21
  231.8 2.9 fusion.23
  234.7 7.8 %collective-permute-done.2 = bf16[8,1,96,720]{3,2,0,1:T(8,128)(2,1)} collective-permute-done((bf16[8,1,96,720]{3,2,0,1:T(8,128)(2,1)S(1)}, bf16[8,1,96,720]{3,2,0,1:T(8,128)(2,1)}, u32[]{:S(2)}, u32[]{:S(2)}) %collective-permute-start.2) | collective-permute-done | bytes 1105952 | tf_op jit(solution)/shard_map/ppermute | solution.py:20
  242.5 4.1 %fusion.13 = bf16[8,1,96,720]{3,2,1,0:T(8,128)(2,1)} fusion(f32[720,8,96]{0,2,1:T(8,128)S(1)} %fusion.21, f32[720,8,96]{0,2,1:T(8,128)S(1)} %fusion.25, f32[720,8,96]{0,2,1:T(8,128)S(1)} %fusion.23, bf16[8,1,96,720]{3,2,0,1:T(8,128)(2,1)} %collective-permute-done.2, bf16[1,2880,720]{1,2,0:T(8,128)(2,1)} %param.24, s32[]{:T(128)S(6)} %select_n.73), kind=kOutput, calls=%fused_computation.16 | convolution fusion | flops 798474240 | bytes 10027012 | tf_op jit(solution)/shard_map/gecf,efd->gecd/dot_general | solution.py:169
  246.6 5.4 %all-to-all-start.1 = ((bf16[8,1,96,720]{3,2,1,0:T(8,128)(2,1)}), bf16[8,1,96,720]{3,2,1,0:T(8,128)(2,1)}, u32[]{:S(2)}, u32[]{:S(2)}) async-start(bf16[8,1,96,720]{3,2,1,0:T(8,128)(2,1)} %fusion.13), calls=%async_computation.1 | async-start | bytes 2359296 | tf_op jit(solution)/shard_map/all_to_all | solution.py:176
  252.1 0.3 fusion.44
  252.4 6.1 %psum.23 = f32[96,8]{0,1:T(8,128)S(1)} all-reduce(f32[96,8]{0,1:T(8,128)S(1)} %fusion.44), channel_id=1, replica_groups=mesh['dp'=8,'tp'=4] {'tp'}, use_global_device_ids=true, to_apply=%region_10.11 | all-reduce | flops 768 | bytes 6144 | tf_op jit(solution)/shard_map/psum | solution.py:127
  258.5 0.2 select_reduce_fusion
  258.7 19.6 %all-to-all-done.1 = bf16[8,1,96,720]{3,2,1,0:T(8,128)(2,1)} async-done(((bf16[8,1,96,720]{3,2,1,0:T(8,128)(2,1)}), bf16[8,1,96,720]{3,2,1,0:T(8,128)(2,1)}, u32[]{:S(2)}, u32[]{:S(2)}) %all-to-all-start.1) | async-done | bytes 1105952 | tf_op jit(solution)/shard_map/all_to_all | solution.py:176
  278.3 2.7 convolution_add_fusion
  (44 shorter events, 0.7 us)
Async XLA Ops:
  6.5 57.3 %copy-start = (bf16[512,2880]{0,1:T(8,128)(2,1)S(1)}, bf16[512,2880]{0,1:T(8,128)(2,1)}, u32[]{:S(2)}) copy-start(bf16[512,2880]{0,1:T(8,128)(2,1)} %param.18) | copy-start | bytes 8847364
  6.5 21.1 %copy-start.7 = (s32[96]{0:T(128)S(1)}, s32[96]{0:T(128)}, u32[]{:S(2)}) copy-start(s32[96]{0:T(128)} %param.20) | copy-start | bytes 1156
  6.5 85.6 %reduce-scatter.4.cloned.1.call-start = ((), (), s32[]{:S(2)}) async-start(), calls=%async_computation.4 | async-start | bytes 921600
  27.6 7.7 %copy-start.4 = (bf16[2880,96,1]{0,1,2:T(8,128)(2,1)S(1)}, bf16[2880,96,1]{0,1,2:T(8,128)(2,1)}, u32[]{:S(2)}) copy-start(bf16[2880,96,1]{0,1,2:T(8,128)(2,1)} %reshape.278) | copy-start | bytes 1658884
  40.4 8.7 %copy-start.3 = (bf16[2880,96]{0,1:T(8,128)(2,1)S(1)}, bf16[2880,96]{0,1:T(8,128)(2,1)}, u32[]{:S(2)}) copy-start(bf16[2880,96]{0,1:T(8,128)(2,1)} %reshape.277) | copy-start | bytes 1658884
  49.1 3.5 %copy-start.9 = (f32[8]{0:T(128)S(1)}, f32[8]{0:T(128)}, u32[]{:S(2)}) copy-start(f32[8]{0:T(128)} %param.17) | copy-start | bytes 100
  52.7 7.2 %copy-start.6 = (pred[96,128]{1,0:T(8,128)(4,1)S(1)}, pred[96,128]{1,0:T(8,128)(4,1)}, u32[]{:S(2)}) copy-start(pred[96,128]{1,0:T(8,128)(4,1)} %fusion.57) | copy-start | bytes 36868
  63.8 4.2 %copy-start.5 = (s32[96,4]{0,1:T(4,128)S(1)}, s32[96,4]{0,1:T(4,128)}, u32[]{:S(2)}) copy-start(s32[96,4]{0,1:T(4,128)} %param.25) | copy-start | bytes 4612
  63.8 29.4 %copy-start.2 = (bf16[96,720]{1,0:T(8,128)(2,1)S(1)}, bf16[96,720]{1,0:T(8,128)(2,1)}, u32[]{:S(2)}) copy-start(bf16[96,720]{1,0:T(8,128)(2,1)} %param.13) | copy-start | bytes 414724
  67.9 110.5 %all-gather.3.cloned.1.call-start = ((), (), s32[]{:S(2)}) async-start(), calls=%async_computation.3 | async-start | bytes 7372800 | tf_op jit(solution)/shard_map/all_gather | solution.py:147
  199.1 27.7 %collective-permute-start.1 = (bf16[8,1,96,720]{3,2,0,1:T(8,128)(2,1)S(1)}, bf16[8,1,96,720]{3,2,0,1:T(8,128)(2,1)S(1)}, u32[]{:S(2)}, u32[]{:S(2)}) collective-permute-start(bf16[8,1,96,720]{3,2,0,1:T(8,128)(2,1)S(1)} %fusion.10), channel_id=1, source_target_pairs={{0,1},{1,2},{2,3},{3,0},{4,5},{5,6},{6,7},{7,4},{8,9},{9,10},{10,1... | collective-permute-start | bytes 3317768 | tf_op jit(solution)/shard_map/ppermute | solution.py:20
  199.4 32.4 %collective-permute-start = (bf16[8,1,96,720]{3,2,0,1:T(8,128)(2,1)S(1)}, bf16[8,1,96,720]{3,2,0,1:T(8,128)(2,1)}, u32[]{:S(2)}, u32[]{:S(2)}) collective-permute-start(bf16[8,1,96,720]{3,2,0,1:T(8,128)(2,1)S(1)} %fusion.10), channel_id=1, source_target_pairs={{0,3},{1,0},{2,1},{3,2},{4,7},{5,4},{6,5},{7,6},{8,11},{9,8},{10,9... | collective-permute-start | bytes 3317768 | tf_op jit(solution)/shard_map/ppermute | solution.py:22
  226.8 15.7 %collective-permute-start.2 = (bf16[8,1,96,720]{3,2,0,1:T(8,128)(2,1)S(1)}, bf16[8,1,96,720]{3,2,0,1:T(8,128)(2,1)}, u32[]{:S(2)}, u32[]{:S(2)}) collective-permute-start(bf16[8,1,96,720]{3,2,0,1:T(8,128)(2,1)S(1)} %collective-permute-done.1), channel_id=1, source_target_pairs={{0,1},{1,2},{2,3},{3,0},{4,5},{5,6},{6,7},{7,4},{8,9},{9,10},{10,1... | collective-permute-start | bytes 3317768 | tf_op jit(solution)/shard_map/ppermute | solution.py:20
  242.5 38.5 %copy-start.1 = (bf16[512,2880]{0,1:T(8,128)(2,1)S(1)}, bf16[512,2880]{0,1:T(8,128)(2,1)}, u32[]{:S(2)}) copy-start(bf16[512,2880]{0,1:T(8,128)(2,1)} %param.18) | copy-start | bytes 8847364
  246.6 5.4 %copy-start.8 = (bf16[720,8]{0,1:T(8,128)(2,1)S(1)}, bf16[720,8]{0,1:T(8,128)(2,1)}, u32[]{:S(2)}) copy-start(bf16[720,8]{0,1:T(8,128)(2,1)} %param.22) | copy-start | bytes 34564
  246.6 31.7 %all-to-all-start.1 = ((bf16[8,1,96,720]{3,2,1,0:T(8,128)(2,1)}), bf16[8,1,96,720]{3,2,1,0:T(8,128)(2,1)}, u32[]{:S(2)}, u32[]{:S(2)}) async-start(bf16[8,1,96,720]{3,2,1,0:T(8,128)(2,1)} %fusion.13), calls=%async_computation.1 | async-start | bytes 2359296 | tf_op jit(solution)/shard_map/all_to_all | solution.py:176
Sparse Core Ops, SparseCore 0:
  68.0 24.0 reduce-scatter.3
  136.6 41.8 all-gather.2
